TPU v7x, 512 devices: a whole 4x4x16 slice. The times are simulated.
512 devices in a mesh: sym: 8 (over y, core), tile: 64 (over z, x).
Axes of the slice: x: 4, y: 4, z: 16, core: 2. Of those that a mesh axis runs over, the one named last changes fastest.
Arguments:
- amplitudes: bfloat16 [256, 131072], P(None, ('sym', 'tile')), may hold values from -6 to 6
- slot_cols: int32 [1024, 64], P(('sym', 'tile')), may hold values from 0 to 127, as said below
- slot_count: int32 [1024], P(('sym', 'tile')), may hold values from 16 to 64, as said below
- integrals: bfloat16 [1024, 64, 128, 128], P(('sym', 'tile')), may hold values from -0.0625 to 0.0625
- cycle_same: bfloat16 [8, 128, 128], P('sym'), may hold values from -0.375 to 0.375
- cycle_cross: bfloat16 [8, 128, 128], P('sym'), may hold values from -0.375 to 0.375
Outputs:
- residual: bfloat16 [256, 131072], P(None, ('sym', 'tile'))
Inputs may be any that keep to these rules, and one draw needn't show every extreme that they name: `slot_cols`: tile index within the symmetry block; the live entries of a row are distinct and rising. `slot_count`: some virtual-pair tile has all 64 slots live.
All inputs are finite; a program needn't handle non-finite values.
Results may differ from a plain program's by a relative error of at most 0.0044.
Values may be sent and summed in bfloat16 or wider, within the bound.
A program may use at most 128 MiB of HBM per device.

v0:
```python
import jax
import jax.numpy as jnp
from jax import lax
from jax.sharding import PartitionSpec as P


def from_partner(value, axis, bit):
    mask = 2**bit
    pairs = [(source, source ^ mask) for source in range(lax.axis_size(axis))]
    return lax.ppermute(value, axis, pairs)


def cycle_rows(same_rows, cross_rows, own_part, other_part, block_tiles, tile_width):
    items = own_part.shape[0]
    own_three = own_part.reshape(items, block_tiles, tile_width)
    other_three = other_part.reshape(items, block_tiles, tile_width)
    result = jnp.einsum("uv,pva->pua", same_rows, own_three, preferred_element_type=jnp.float32)
    result = result + jnp.einsum(
        "uv,pva->pua", cross_rows, other_three, preferred_element_type=jnp.float32
    )
    return result


def on_device(amplitudes, slot_cols, slot_count, integrals, cycle_same, cycle_cross):
    pair_count = amplitudes.shape[0]
    rows_local = integrals.shape[0]
    slot_total = integrals.shape[1]
    tile_width = integrals.shape[3]
    block_tiles = cycle_same.shape[1]
    gathered = lax.all_gather(amplitudes, "tile", axis=1, tiled=True)
    block_three = gathered.reshape(pair_count, block_tiles, tile_width)
    live_slot = lax.broadcasted_iota(jnp.int32, (rows_local, slot_total), 1) < slot_count[:, None]
    take_index = jnp.where(live_slot, slot_cols, block_tiles)
    ladder_parts = []
    for tile_row in range(rows_local):
        picked = jnp.take(block_three, take_index[tile_row], axis=1, mode="fill", fill_value=0)
        ladder_parts.append(
            jnp.einsum(
                "psc,sac->pa", picked, integrals[tile_row], preferred_element_type=jnp.float32
            )
        )
    ladder = jnp.stack(ladder_parts, axis=1).reshape(pair_count, rows_local * tile_width)
    dressed = (amplitudes.astype(jnp.float32) + ladder).astype(jnp.bfloat16)
    partner = from_partner(dressed, "sym", 0)
    whole_own, whole_partner = (
        lax.all_gather(dressed, "tile", axis=1, tiled=True),
        lax.all_gather(partner, "tile", axis=1, tiled=True),
    )
    position = lax.axis_index("tile")
    same_rows = lax.dynamic_slice_in_dim(cycle_same[0], position * rows_local, rows_local, 0)
    cross_rows = lax.dynamic_slice_in_dim(cycle_cross[0], position * rows_local, rows_local, 0)
    cycle_term = cycle_rows(
        same_rows, cross_rows, whole_own, whole_partner, block_tiles, tile_width
    )
    cycle_term = cycle_term.reshape(pair_count, rows_local * tile_width)
    return (ladder + cycle_term).astype(jnp.bfloat16)


def solution(mesh):
    in_specs = (
        P(None, ("sym", "tile")),
        P(("sym", "tile"), None),
        P(("sym", "tile")),
        P(("sym", "tile"), None, None, None),
        P("sym", None, None),
        P("sym", None, None),
    )
    out_specs = P(None, ("sym", "tile"))
    return jax.shard_map(
        on_device, mesh=mesh, in_specs=in_specs, out_specs=out_specs, check_vma=False
    )
```

profile of v0, /device:TPU:8, one launch (start us, length us, event | category | flops | bytes accessed | tf_op | source)
XLA Modules:
  0.0 553.8 jit_solution(9314749196532757080)
XLA Ops:
  6.5 0.0 copy-start
  6.5 0.0 all-gather.4.cloned.1.call-start
  6.5 1.7 copy.11
  8.2 0.0 all-gather.4.cloned.1.call-update
  8.2 0.0 all-gather.6.cloned.1.call-start
  8.3 0.8 compare_select_fusion.2
  9.1 161.6 %all-gather.4.cloned.1.call-done = bf16[256,16384]{0,1:T(8,128)(2,1)} async-done(((bf16[256,256]{0,1:T(8,128)(2,1)}), bf16[256,16384]{0,1:T(8,128)(2,1)}) %all-gather.4.cloned.1.call-update) | async-done | bytes 8388624 | tf_op jit(solution)/shard_map/all_gather | solution.py:30
  170.7 12.0 %copy.12 = bf16[256,128,128]{2,0,1:T(8,128)(2,1)} copy(bf16[256,128,128]{0,2,1:T(8,128)(2,1)} %bitcast.58) | data formatting | bytes 16777216 | tf_op jit(solution)/shard_map/reshape | solution.py:31
  182.7 6.4 %gather_fusion.1 = bf16[64,256,128]{2,1,0:T(8,128)(2,1)} fusion(bf16[256,128,128]{2,0,1:T(8,128)(2,1)} %copy.12, s32[1024]{0:T(1024)S(1)} %get-tuple-element.12), kind=kCustom, calls=%fused_computation.1.clone | custom fusion | bytes 8388864 | tf_op jit(solution)/shard_map/jit(_take)/gather | solution.py:36
  189.1 6.4 %gather_fusion = bf16[64,256,128]{2,1,0:T(8,128)(2,1)} fusion(bf16[256,128,128]{2,0,1:T(8,128)(2,1)} %copy.12, s32[1024]{0:T(1024)S(1)} %get-tuple-element.13), kind=kCustom, calls=%fused_computation.clone | custom fusion | bytes 8388864 | tf_op jit(solution)/shard_map/jit(_take)/gather | solution.py:36
  195.5 0.0 copy-start.1
  195.5 4.6 fusion.14
  200.1 0.0 copy-done.1
  200.1 0.8 copy-done.4
  200.8 1.6 fusion.19
  202.4 0.1 copy.15
  202.6 0.0 copy-done.2
  202.6 0.7 add_convert_fusion
  203.3 0.0 all-gather.6.cloned.1.call-update
  203.3 0.0 all-gather.8.cloned.1.call-start
  203.3 1.9 collective-permute-start
  205.3 1.5 collective-permute-done
  206.8 0.6 copy-done.3
  207.4 0.0 all-gather.8.cloned.1.call-update
  207.5 159.4 %all-gather.6.cloned.1.call-done = bf16[256,16384]{1,0:T(8,128)(2,1)} async-done(((bf16[256,256]{1,0:T(8,128)(2,1)}), bf16[256,16384]{1,0:T(8,128)(2,1)}) %all-gather.6.cloned.1.call-update) | async-done | bytes 8388624 | tf_op jit(solution)/shard_map/all_gather | solution.py:46
  366.8 9.2 %copy.16 = bf16[32,8,128,128]{3,2,1,0:T(8,128)(2,1)} copy(bf16[32,8,128,128]{3,1,2,0:T(8,128)(2,1)} %bitcast.56) | data formatting | bytes 16777216
  376.0 0.0 copy-done
  376.0 4.6 fusion.26
  380.6 152.2 %all-gather.8.cloned.1.call-done = bf16[256,16384]{1,0:T(8,128)(2,1)} async-done(((bf16[256,256]{1,0:T(8,128)(2,1)}), bf16[256,16384]{1,0:T(8,128)(2,1)}) %all-gather.8.cloned.1.call-update) | async-done | bytes 8388624 | tf_op jit(solution)/shard_map/all_gather | solution.py:47
  532.8 9.2 %copy.17 = bf16[32,8,128,128]{3,2,1,0:T(8,128)(2,1)} copy(bf16[32,8,128,128]{3,1,2,0:T(8,128)(2,1)} %bitcast.57) | data formatting | bytes 16777216
  542.0 4.6 convolution_add_fusion
  546.6 0.7 fusion.24
  (6 shorter events, 0.0 us)
Async XLA Ops:
  6.5 369.5 %copy-start = (bf16[1,128,128]{2,1,0:T(8,128)(2,1)S(1)}, bf16[1,128,128]{2,1,0:T(8,128)(2,1)}, u32[]{:S(2)}) copy-start(bf16[1,128,128]{2,1,0:T(8,128)(2,1)} %param.12) | copy-start | bytes 98308
  6.5 164.1 %all-gather.4.cloned.1.call-start = ((), (), s32[]{:S(2)}) async-start(), calls=%async_computation | async-start | bytes 8519680 | tf_op jit(solution)/shard_map/all_gather | solution.py:30
  8.2 358.6 %all-gather.6.cloned.1.call-start = ((), (), s32[]{:S(2)}) async-start(), calls=%async_computation.1 | async-start | bytes 8519680 | tf_op jit(solution)/shard_map/all_gather | solution.py:46
  195.5 4.6 copy-start.1
  195.5 5.3 copy-start.4
  200.8 1.7 copy-start.2
  203.3 329.5 %all-gather.8.cloned.1.call-start = ((), (), s32[]{:S(2)}) async-start(), calls=%async_computation.2 | async-start | bytes 8519680 | tf_op jit(solution)/shard_map/all_gather | solution.py:47
  203.3 3.5 collective-permute-start
  206.8 0.6 copy-start.3
Sparse Core Ops, SparseCore 0:
  10.3 160.3 all-gather.3
  203.4 163.3 all-gather.5
  369.7 163.0 all-gather.7
where the time goes:
time: 554 us
  waiting for transfers between devices  475 us (86%)
  local copies, waits for them, and re-layouts  46.4 us (8%)
  matrix products  15.3 us (3%)
  between operations  13.2 us (2%)
    all_gather x1, waiting for transfers between devices, on_device(): gathered = lax.all_gather(amplitudes, 'tile', axis=1, tiled=True)  162 us
    all_gather x1, waiting for transfers between devices, on_device(): lax.all_gather(dressed, 'tile', axis=1, tiled=True)  159 us
    all_gather x1, waiting for transfers between devices, on_device(): lax.all_gather(partner, 'tile', axis=1, tiled=True)  152 us
    unnamed x13, local copies, waits for them, and re-layouts  21.5 us
    gather x2, local copies, waits for them, and re-layouts, on_device(): jnp.take(block_three, take_index[tile_row], axis=1, mode='fill', fill_val...  12.8 us
    reshape x1, local copies, waits for them, and re-layouts, on_device(): block_three = gathered.reshape(pair_count, block_tiles, tile_width)  12 us
  transfers between devices with their start and end apart: 4, of which 4 were waited for; matrix products, arithmetic and copies ran while one was open for 3% of the time, Pallas kernels for 0%

commit v1 on v0

--- a/solution.py
+++ b/solution.py
@@ -43,7 +43,9 @@
     dressed = (amplitudes.astype(jnp.float32) + ladder).astype(jnp.bfloat16)
     partner = from_partner(dressed, "sym", 0)
     whole_own, whole_partner = (
-        lax.all_gather(dressed, "tile", axis=1, tiled=True),
+        jnp.concatenate(
+            lax.all_to_all(jnp.stack([dressed] * lax.axis_size("tile")), "tile", 0, 0), axis=1
+        ),
         lax.all_gather(partner, "tile", axis=1, tiled=True),
     )
     position = lax.axis_index("tile")

time: 554 us -> 685 us (1.24)
  the two profiles are of different devices: /device:TPU:8 before, /device:TPU:68 now
where the time goes in v1:
time: 685 us
  waiting for transfers between devices  575 us (84%)
  local copies, waits for them, and re-layouts  65.7 us (10%)
  matrix products  15.3 us (2%)
  starting transfers between devices  13.6 us (2%)
  between operations  13.5 us (2%)
    all_gather x1, waiting for transfers between devices, on_device(): lax.all_gather(partner, 'tile', axis=1, tiled=True)  415 us
    all_gather x1, waiting for transfers between devices, on_device(): gathered = lax.all_gather(amplitudes, 'tile', axis=1, tiled=True)  159 us
  transfers between devices with their start and end apart: 4, of which 3 were waited for; matrix products, arithmetic and copies ran while one was open for 1% of the time, Pallas kernels for 0%

profile of v1, /device:TPU:68, one launch (start us, length us, event | category | flops | bytes accessed | tf_op | source)
XLA Modules:
  0.0 684.5 jit_solution(16179702592387552782)
XLA Ops:
  6.5 0.0 copy-start
  6.5 0.0 all-gather.3.cloned.1.call-start
  6.5 1.7 copy.16
  8.2 0.0 all-gather.3.cloned.1.call-update
  8.2 0.8 compare_select_fusion.2
  9.0 158.9 %all-gather.3.cloned.1.call-done = bf16[256,16384]{0,1:T(8,128)(2,1)} async-done(((bf16[256,256]{0,1:T(8,128)(2,1)}), bf16[256,16384]{0,1:T(8,128)(2,1)}) %all-gather.3.cloned.1.call-update) | async-done | bytes 8388624 | tf_op jit(solution)/shard_map/all_gather | solution.py:30
  167.9 12.0 %copy.17 = bf16[256,128,128]{2,0,1:T(8,128)(2,1)} copy(bf16[256,128,128]{0,2,1:T(8,128)(2,1)} %bitcast.55) | data formatting | bytes 16777216 | tf_op jit(solution)/shard_map/reshape | solution.py:31
  179.9 6.4 gather_fusion
  186.3 6.4 gather_fusion.1
  192.7 0.0 copy-start.1
  192.7 4.6 fusion.14
  197.3 0.0 copy-done.1
  197.3 0.8 copy-done.4
  198.0 1.6 fusion.19
  199.6 0.1 copy.21
  199.8 0.0 copy-done.2
  199.8 4.2 stack.11
  204.0 11.5 %all-to-all-start = ((bf16[64,256,256]{2,1,0:T(8,128)(2,1)}), bf16[64,256,256]{2,1,0:T(8,128)(2,1)}, u32[]{:S(2)}, u32[]{:S(2)}) async-start(bf16[64,256,256]{2,1,0:T(8,128)(2,1)} %stack.11), calls=%async_computation | async-start | bytes 16777216 | tf_op jit(solution)/shard_map/all_to_all | solution.py:47
  215.5 0.0 all-gather.5.cloned.1.call-start
  215.6 2.1 collective-permute-start
  217.7 1.1 collective-permute-done
  218.8 0.7 copy-done.3
  219.5 0.0 all-gather.5.cloned.1.call-update
  219.5 414.8 %all-gather.5.cloned.1.call-done = bf16[256,16384]{1,0:T(8,128)(2,1)} async-done(((bf16[256,256]{1,0:T(8,128)(2,1)}), bf16[256,16384]{1,0:T(8,128)(2,1)}) %all-gather.5.cloned.1.call-update) | async-done | bytes 8388624 | tf_op jit(solution)/shard_map/all_gather | solution.py:49
  634.3 9.2 %copy.22 = bf16[32,8,128,128]{3,2,1,0:T(8,128)(2,1)} copy(bf16[32,8,128,128]{3,1,2,0:T(8,128)(2,1)} %bitcast.54) | data formatting | bytes 16777216
  643.5 0.0 all-to-all-done
  643.5 11.4 %copy.20 = bf16[256,64,256]{2,1,0:T(8,128)(2,1)} copy(bf16[256,64,256]{2,0,1:T(8,128)(2,1)} %bitcast.12) | data formatting | bytes 16777216 | tf_op jit(solution)/shard_map/reshape | solution.py:46
  654.9 12.9 %reshape_reshape.3 = bf16[256,128,128]{2,1,0:T(8,128)(2,1)} reshape(bf16[256,64,256]{2,1,0:T(8,128)(2,1)} %copy.20) | data formatting | bytes 16777216 | tf_op jit(solution)/shard_map/reshape;reshape | solution.py:15
  667.8 0.0 copy-done
  667.8 4.6 fusion.26
  672.4 4.6 convolution_add_fusion
  677.0 0.7 fusion.24
  (7 shorter events, 0.1 us)
Async XLA Ops:
  6.5 661.3 %copy-start = (bf16[1,128,128]{2,1,0:T(8,128)(2,1)S(1)}, bf16[1,128,128]{2,1,0:T(8,128)(2,1)}, u32[]{:S(2)}) copy-start(bf16[1,128,128]{2,1,0:T(8,128)(2,1)} %param.12) | copy-start | bytes 98308
  6.5 161.4 %all-gather.3.cloned.1.call-start = ((), (), s32[]{:S(2)}) async-start(), calls=%async_computation.1 | async-start | bytes 8519680 | tf_op jit(solution)/shard_map/all_gather | solution.py:30
  192.7 4.6 copy-start.1
  192.7 5.3 copy-start.4
  198.0 1.7 copy-start.2
  204.0 439.5 %all-to-all-start = ((bf16[64,256,256]{2,1,0:T(8,128)(2,1)}), bf16[64,256,256]{2,1,0:T(8,128)(2,1)}, u32[]{:S(2)}, u32[]{:S(2)}) async-start(bf16[64,256,256]{2,1,0:T(8,128)(2,1)} %stack.11), calls=%async_computation | async-start | bytes 16777216 | tf_op jit(solution)/shard_map/all_to_all | solution.py:47
  215.5 418.8 %all-gather.5.cloned.1.call-start = ((), (), s32[]{:S(2)}) async-start(), calls=%async_computation.2 | async-start | bytes 8519680 | tf_op jit(solution)/shard_map/all_gather | solution.py:49
  215.6 3.2 collective-permute-start
  218.8 0.7 copy-start.3
Sparse Core Ops, SparseCore 0:
  10.3 157.5 all-gather.2
  219.6 414.6 all-gather.4
